TPU v7x, 1024 devices: a whole 4x8x16 slice. The times are simulated.
1024 devices in a mesh: er: 4 (over z_lo), ec: 4 (over z_hi), dp: 64 (over x, y, core).
Axes of the slice: x: 4, y: 8, z: 16 (z_hi: 4, z_lo: 4; z = z_hi * 4 + z_lo), core: 2. Of those that a mesh axis runs over, the one named last changes fastest.
Arguments:
- out_grad: bfloat16 [64, 1024, 4096], P('dp', 'er', 'ec'), may hold values from -6 to 6
- route_probs: float32 [64, 1024], P('dp', 'er'), may hold values from 0.1 to 1
- expert_ids: int32 [64, 1024], P('dp', 'er'), may hold values from 0 to 3, as said below
- slot_ids: int32 [64, 1024], P('dp', 'er'), may hold values from 0 to 71, as said below
- gate_pre: bfloat16 [64, 4, 288, 768], P('dp', 'er'), may hold values from -6 to 6
- up_act: bfloat16 [64, 4, 288, 768], P('dp', 'er'), may hold values from -6 to 6
- w_gate: bfloat16 [4, 4096, 768], P('er', 'ec'), may hold values from -0.09375 to 0.09375
- w_up: bfloat16 [4, 4096, 768], P('er', 'ec'), may hold values from -0.09375 to 0.09375
- w_down: bfloat16 [4, 768, 4096], P('er', None, 'ec'), may hold values from -0.21875 to 0.21875
Outputs:
- input_grad: bfloat16 [64, 1024, 4096], P('dp', 'er', 'ec')
- down_grad: float32 [4, 768, 4096], P('er', 'dp', 'ec')
Inputs may be any that keep to these rules, and one draw needn't show every extreme that they name: `expert_ids`: within each group of 256 tokens no expert is chosen by more than 72 tokens; in every replica some expert is chosen by exactly 72 tokens of every group of that replica. `slot_ids`: tokens of one group that chose the same expert have distinct slots.
All inputs are finite; a program needn't handle non-finite values.
Results may differ from a plain program's by a relative error of at most 0.015.
Values may be sent and summed in bfloat16 or wider, within the bound.
A program may use at most 64 MiB of HBM per device.

v0:
```python
import jax
import jax.numpy as jnp
from jax import lax
from jax.sharding import PartitionSpec as P


def cut_along(x, dim, size):
    before, after = (x.shape[:dim], x.shape[dim + 1 :])
    return jnp.moveaxis(x.reshape(*before, size, -1, *after), dim, 0)


def sum_at_owner(x, axis, dim):
    size = lax.axis_size(axis)
    tiles = lax.all_to_all(cut_along(x, dim, size), axis, 0, 0, tiled=True)
    return jnp.sum(tiles, axis=0)


def from_everyone(x, axis):
    copies = jnp.broadcast_to(x, (lax.axis_size(axis), *x.shape))
    return lax.all_to_all(copies, axis, split_axis=0, concat_axis=0, tiled=True)


def over_copies(x, axis):
    everything = from_everyone(x, axis)
    return jnp.sum(everything.astype(jnp.float32), axis=0)


def swiglu_grads(hid_grad, pre_rows, up_rows):
    pre_float = pre_rows.astype(jnp.float32)
    up_float = up_rows.astype(jnp.float32)
    sigmoid = jax.nn.sigmoid(pre_float)
    gate_grad = (hid_grad * up_float * sigmoid * (1.0 + pre_float * (1.0 - sigmoid))).astype(
        jnp.bfloat16
    )
    up_grad = (hid_grad * pre_float * sigmoid).astype(jnp.bfloat16)
    return (gate_grad, up_grad)


def reduce_weights(hidden, arrived):
    replicas = lax.axis_size("dp")
    summed = sum_at_owner(
        lax.dot_general(
            hidden, arrived, (((0,), (0,)), ((), ())), preferred_element_type=jnp.float32
        ),
        "dp",
        0,
    )
    return summed / replicas


def body(out_grad, route_probs, expert_ids, slot_ids, gate_pre, up_act, w_gate, w_up, w_down):
    tokens = out_grad[0]
    experts = lax.axis_size("er")
    capacity = gate_pre.shape[2] // experts
    slot_count = experts * capacity
    position = expert_ids[0] * capacity + slot_ids[0]
    scaled = (route_probs[0][:, None] * tokens.astype(jnp.float32)).astype(jnp.bfloat16)
    source = (
        jnp.zeros((slot_count,), jnp.int32)
        .at[position]
        .set(jnp.arange(tokens.shape[0], dtype=jnp.int32))
    )
    filled = jnp.zeros((slot_count,), jnp.bool_).at[position].set(True)
    outgoing = jnp.where(filled[:, None], scaled[source], jnp.zeros((), jnp.bfloat16))
    arrived = lax.all_to_all(outgoing, "er", split_axis=0, concat_axis=0, tiled=True)
    pre_rows = gate_pre[0, 0]
    up_rows = up_act[0, 0]
    pre_float = pre_rows.astype(jnp.float32)
    hidden = (pre_float * jax.nn.sigmoid(pre_float) * up_rows.astype(jnp.float32)).astype(
        jnp.bfloat16
    )
    partial_value = lax.dot_general(
        arrived, w_down[0], (((1,), (1,)), ((), ())), preferred_element_type=jnp.float32
    )
    hid_grad = over_copies(partial_value.astype(jnp.bfloat16), "ec").astype(jnp.float32)
    gate_grad, up_grad = swiglu_grads(hid_grad, pre_rows, up_rows)
    slot_grad = (
        lax.dot_general(
            gate_grad, w_gate[0], (((1,), (1,)), ((), ())), preferred_element_type=jnp.float32
        )
        + lax.dot_general(
            up_grad, w_up[0], (((1,), (1,)), ((), ())), preferred_element_type=jnp.float32
        )
    ).astype(jnp.bfloat16)
    returned = lax.all_to_all(slot_grad, "er", split_axis=0, concat_axis=0, tiled=True)
    down_part = reduce_weights(hidden, arrived)
    input_grad = returned[position]
    return (input_grad[None], down_part[None])


def solution(mesh):
    in_specs = (
        P("dp", "er", "ec"),
        P("dp", "er"),
        P("dp", "er"),
        P("dp", "er"),
        P("dp", "er", None, None),
        P("dp", "er", None, None),
        P("er", "ec", None),
        P("er", "ec", None),
        P("er", None, "ec"),
    )
    out_specs = (P("dp", "er", "ec"), P("er", "dp", "ec"))
    return jax.shard_map(body, mesh=mesh, in_specs=in_specs, out_specs=out_specs, check_vma=False)
```

profile of v0, /device:TPU:1, one launch (start us, length us, event | category | flops | bytes accessed | tf_op | source)
XLA Modules:
  0.0 263.1 jit_solution(18025666077872962681)
XLA Ops:
  0.6 0.0 copy-start
  0.6 0.8 compare_select_fusion
  1.5 1.5 scatter_custom_fusion
  3.0 0.1 broadcast_in_dim.36
  3.1 1.4 scatter_custom_fusion.1
  4.5 1.2 fusion.17
  5.7 2.1 gather_fusion
  7.8 0.0 copy-start.4
  7.8 0.1 broadcast_select_fusion
  7.9 17.6 %all_to_all.31 = bf16[4,72,1024]{2,1,0:T(8,128)(2,1)S(1)} all-to-all(bf16[4,72,1024]{2,1,0:T(8,128)(2,1)S(1)} %broadcast_select_fusion), channel_id=1, replica_groups=mesh['er'=4,'ec'=4,'dp'=64] {'er'}, dimensions={0} | all-to-all | bytes 1179648 | tf_op jit(solution)/shard_map/all_to_all | solution.py:65
  25.5 0.0 copy-start.1
  25.5 0.8 copy-done.1
  26.3 0.0 copy-done.4
  26.3 0.7 fusion.12
  27.0 1.4 broadcast_in_dim.40
  28.3 21.3 %all-to-all-start.1 = ((bf16[4,288,768]{2,1,0:T(8,128)(2,1)}), bf16[4,288,768]{2,1,0:T(8,128)(2,1)S(1)}, u32[]{:S(2)}, u32[]{:S(2)}) async-start(bf16[4,288,768]{2,1,0:T(8,128)(2,1)} %broadcast_in_dim.40), calls=%async_computation.1 | async-start | bytes 3538944 | tf_op jit(solution)/shard_map/all_to_all | solution.py:20
  49.6 2.2 fusion.38
  51.8 2.1 copy.17
  53.9 2.1 dot_general.20
  56.1 2.3 fusion.32
  58.3 3.8 %copy.19 = f32[64,12,1024]{2,1,0:T(8,128)} copy(f32[64,12,1024]{2,0,1:T(8,128)S(1)} %fusion.32) | data formatting | bytes 6291456 | tf_op jit(solution)/shard_map/dot_general | solution.py:42
  62.1 69.2 %all-to-all-done.1 = bf16[4,288,768]{2,1,0:T(8,128)(2,1)S(1)} async-done(((bf16[4,288,768]{2,1,0:T(8,128)(2,1)}), bf16[4,288,768]{2,1,0:T(8,128)(2,1)S(1)}, u32[]{:S(2)}, u32[]{:S(2)}) %all-to-all-start.1) | async-done | bytes 1769504 | tf_op jit(solution)/shard_map/all_to_all | solution.py:20
  131.4 14.7 %all-to-all-start.3 = ((f32[64,12,1024]{2,1,0:T(8,128)}), f32[64,12,1024]{2,1,0:T(8,128)}, u32[]{:S(2)}, u32[]{:S(2)}) async-start(f32[64,12,1024]{2,1,0:T(8,128)} %copy.19), calls=%async_computation.3 | async-start | bytes 8388608 | tf_op jit(solution)/shard_map/all_to_all | solution.py:14
  146.1 0.0 copy-start.2
  146.1 0.2 convert_reduce_fusion
  146.4 0.0 copy-done
  146.4 0.8 copy-done.2
  147.1 0.0 copy-start.3
  147.1 0.0 copy-start.5
  147.1 0.7 fusion
  147.8 0.3 copy-done.3
  148.1 0.5 copy-done.5
  148.7 1.7 fusion.9
  150.4 91.6 %all-to-all-done.3 = f32[64,12,1024]{2,1,0:T(8,128)} async-done(((f32[64,12,1024]{2,1,0:T(8,128)}), f32[64,12,1024]{2,1,0:T(8,128)}, u32[]{:S(2)}, u32[]{:S(2)}) %all-to-all-start.3) | async-done | bytes 3145760 | tf_op jit(solution)/shard_map/all_to_all | solution.py:14
  242.0 3.5 %all-to-all-start.2 = ((bf16[4,72,1024]{2,1,0:T(8,128)(2,1)}), bf16[4,72,1024]{2,1,0:T(8,128)(2,1)S(1)}, u32[]{:S(2)}, u32[]{:S(2)}) async-start(bf16[4,72,1024]{2,1,0:T(8,128)(2,1)} %bitcast.12), calls=%async_computation.2 | async-start | bytes 1179648 | tf_op jit(solution)/shard_map/all_to_all | solution.py:85
  245.5 2.5 reduce_sum.22
  247.9 0.7 div.20
  248.6 12.6 %all-to-all-done.2 = bf16[4,72,1024]{2,1,0:T(8,128)(2,1)S(1)} async-done(((bf16[4,72,1024]{2,1,0:T(8,128)(2,1)}), bf16[4,72,1024]{2,1,0:T(8,128)(2,1)S(1)}, u32[]{:S(2)}, u32[]{:S(2)}) %all-to-all-start.2) | async-done | bytes 589856 | tf_op jit(solution)/shard_map/all_to_all | solution.py:85
  261.2 2.0 gather_fusion.1
  (6 shorter events, 0.0 us)
Async XLA Ops:
  0.6 145.7 %copy-start = (bf16[1,1024,768]{2,1,0:T(8,128)(2,1)S(1)}, bf16[1,1024,768]{2,1,0:T(8,128)(2,1)}, u32[]{:S(2)}) copy-start(bf16[1,1024,768]{2,1,0:T(8,128)(2,1)} %param.16) | copy-start | bytes 4718596
  7.8 18.5 %copy-start.4 = (bf16[1,768,1024]{2,1,0:T(8,128)(2,1)S(1)}, bf16[1,768,1024]{2,1,0:T(8,128)(2,1)}, u32[]{:S(2)}) copy-start(bf16[1,768,1024]{2,1,0:T(8,128)(2,1)} %param.17) | copy-start | bytes 4718596
  25.5 0.8 copy-start.1
  28.3 103.0 %all-to-all-start.1 = ((bf16[4,288,768]{2,1,0:T(8,128)(2,1)}), bf16[4,288,768]{2,1,0:T(8,128)(2,1)S(1)}, u32[]{:S(2)}, u32[]{:S(2)}) async-start(bf16[4,288,768]{2,1,0:T(8,128)(2,1)} %broadcast_in_dim.40), calls=%async_computation.1 | async-start | bytes 3538944 | tf_op jit(solution)/shard_map/all_to_all | solution.py:20
  131.4 110.6 %all-to-all-start.3 = ((f32[64,12,1024]{2,1,0:T(8,128)}), f32[64,12,1024]{2,1,0:T(8,128)}, u32[]{:S(2)}, u32[]{:S(2)}) async-start(f32[64,12,1024]{2,1,0:T(8,128)} %copy.19), calls=%async_computation.3 | async-start | bytes 8388608 | tf_op jit(solution)/shard_map/all_to_all | solution.py:14
  146.1 1.0 copy-start.2
  147.1 1.0 copy-start.3
  147.1 1.6 copy-start.5
  242.0 19.2 %all-to-all-start.2 = ((bf16[4,72,1024]{2,1,0:T(8,128)(2,1)}), bf16[4,72,1024]{2,1,0:T(8,128)(2,1)S(1)}, u32[]{:S(2)}, u32[]{:S(2)}) async-start(bf16[4,72,1024]{2,1,0:T(8,128)(2,1)} %bitcast.12), calls=%async_computation.2 | async-start | bytes 1179648 | tf_op jit(solution)/shard_map/all_to_all | solution.py:85
where the time goes:
time: 264 us; the launch traced here: 263 us
  waiting for transfers between devices  173 us (66%)
  starting transfers between devices  39.5 us (15%)
  local copies, waits for them, and re-layouts  19.5 us (7%)
  blocking collectives  17.6 us (7%)
  other arithmetic  7.03 us (3%)
  matrix products  5.33 us (2%)
    all_to_all x1, waiting for transfers between devices, sum_at_owner(): tiles = lax.all_to_all(cut_along(x, dim, size), axis, 0, 0, tiled=True)  91.6 us
    all_to_all x1, waiting for transfers between devices, from_everyone(): return lax.all_to_all(copies, axis, split_axis=0, concat_axis=0, tiled=True)  69.2 us
    all_to_all x1, starting transfers between devices, from_everyone(): return lax.all_to_all(copies, axis, split_axis=0, concat_axis=0, tiled=True)  21.3 us
    all_to_all x1, blocking collectives, body(): lax.all_to_all(outgoing, 'er', split_axis=0, concat_axis=0, tiled=True)  17.6 us
    all_to_all x1, starting transfers between devices, sum_at_owner(): tiles = lax.all_to_all(cut_along(x, dim, size), axis, 0, 0, tiled=True)  14.7 us
    all_to_all x1, waiting for transfers between devices, body(): lax.all_to_all(slot_grad, 'er', split_axis=0, concat_axis=0, tiled=True)  12.6 us
    dot_general x3, local copies, waits for them, and re-layouts, reduce_weights(): lax.dot_general(hidden, arrived, (((0,), (0,)), ((), ())), preferred_elem...  8.04 us
  transfers between devices with their start and end apart: 3, of which 3 were waited for; matrix products, arithmetic and copies ran while one was open for 7% of the time, Pallas kernels for 0%

commit v1 on v0

v1 whole, which is shorter than its diff:
```python
import functools

import jax
import jax.numpy as jnp
from jax import lax
from jax.experimental import pallas as pl
from jax.experimental.pallas import tpu as pltpu
from jax.sharding import PartitionSpec as P

MESH = pl.DeviceIdType.MESH
F32, BF16 = jnp.float32, jnp.bfloat16
NX, NY, NC = 4, 8, 2
N = 4


def nt(a, b):
    return lax.dot_general(a, b, (((1,), (1,)), ((), ())), preferred_element_type=F32)


def kernel(
    tok_hbm, prob_ref, ids_ref, slots_ref, gate_hbm, up_hbm, wg_hbm, wu_hbm, wd_hbm,
    out_ref, down_ref,
    tok, gate, up, wg, wu, wd,
    outbuf, arrived, returned, slotbuf,
    gfac, ufac, hidden, hid_t,
    part, own, relay_in, direct_in, comb, comb_in, hid,
    dn, cin, xs, xin, ysum, ys, yin,
    lsem, disp_s, disp_r, rel_s, rel_r, dir_s, dir_r, com_s, com_r,
    aga_s, aga_r, agb_s, agb_r, agf_s, agf_r, ret_s, ret_r,
    core_s, core_r, x_s, x_r, y_s, y_r,
):
    e, c, p = lax.axis_index("er"), lax.axis_index("ec"), lax.axis_index("dp")
    core, y, x = p % NC, (p // NC) % NY, p // (NC * NY)
    cap = arrived.shape[1]
    half = part.shape[3]
    rows12 = ysum.shape[0] // NY

    def dp_at(x2, y2, core2):
        return (x2 * NY + y2) * NC + core2

    loads = [
        pltpu.make_async_copy(s, d, lsem.at[i])
        for i, (s, d) in enumerate(
            [(tok_hbm, tok), (gate_hbm, gate), (up_hbm, up), (wd_hbm, wd), (wg_hbm, wg), (wu_hbm, wu)]
        )
    ]
    for load in loads:
        load.start()

    right, left = {"ec": (c + 1) % N}, {"ec": (c + 3) % N}
    partners = [{"er": (e + k) % N} for k in (1, 2, 3)] + [right, left]
    partners += [{"dp": dp_at(x, y, 1 - core)}]
    partners += [{"dp": dp_at((x + k) % NX, y, core)} for k in range(1, NX)]
    partners += [{"dp": dp_at(x, (y + k) % NY, core)} for k in range(1, NY)]
    barrier = pltpu.get_barrier_semaphore()
    for partner in partners:
        pl.semaphore_signal(barrier, inc=1, device_id=partner, device_id_type=MESH)

    def remote(src, dst, s, r, dev):
        return pltpu.make_async_remote_copy(
            src_ref=src, dst_ref=dst, send_sem=s, recv_sem=r, device_id=dev, device_id_type=MESH
        )

    tokens = tok.shape[0]
    pos_row = ids_ref[...] * cap + slots_ref[...]
    eye = lax.broadcasted_iota(jnp.int32, (tokens, tokens), 0) == lax.broadcasted_iota(
        jnp.int32, (tokens, tokens), 1
    )

    def as_column(row):
        return jnp.sum(jnp.where(eye, jnp.broadcast_to(row, (tokens, tokens)), 0.0), axis=1, keepdims=True)

    prob_col = as_column(prob_ref[...])
    pos_col = as_column(pos_row.astype(F32))
    loads[0].wait()
    tok[...] = (prob_col * tok[...].astype(F32)).astype(BF16)
    for n, d in enumerate((2, 1, 3, 0)):
        dest = (c + d - e + 2 * N) % N
        k = (dest - e + N) % N
        slot = lax.broadcasted_iota(jnp.int32, (cap, tokens), 0) + dest * cap
        pick = jnp.where(slot == pos_row, 1.0, 0.0).astype(BF16)
        outbuf[d] = jnp.dot(pick, tok[...], preferred_element_type=F32).astype(BF16)
        if n == 0:
            pl.semaphore_wait(barrier, len(partners))

        @pl.when(k == 0)
        def _():
            arrived[e] = outbuf[d]

        @pl.when(k != 0)
        def _():
            remote(outbuf.at[d], arrived.at[e], disp_s.at[k - 1], disp_r.at[k - 1], {"er": dest}).start()

    loads[1].wait()
    loads[2].wait()

    def activations(r, _):
        a, u = gate[r].astype(F32), up[r].astype(F32)
        s = jax.nn.sigmoid(a)
        act = a * s
        ufac[r] = act
        gfac[r] = u * s * (1.0 + a * (1.0 - s))
        hidden[r] = (act * u).astype(BF16)
        return 0

    lax.fori_loop(0, N, activations, 0)
    mrows = hid_t.shape[2]
    width = hidden.shape[2]

    def arrange(q, _):
        row = q * mrows + lax.broadcasted_iota(jnp.int32, (mrows, width), 0)
        other = jnp.where(row >= width // 2, 1, 0)
        rem = row - other * (width // 2)
        group = ((rem.astype(F32) + 0.5) * (1.0 / rows12)).astype(jnp.int32)
        source = rem + rows12 * (group + other)
        pick = jnp.where(source == lax.broadcasted_iota(jnp.int32, (mrows, width), 1), 1.0, 0.0).astype(BF16)
        for r in range(N):
            hid_t[q, r] = nt(pick, hidden[r]).astype(BF16)
        return 0

    lax.fori_loop(0, NX * NC, arrange, 0)

    loads[3].wait()

    def partial(d):
        r = (c + d - e + 2 * N) % N
        k = (e - r + N) % N

        @pl.when(k != 0)
        def _():
            remote(outbuf.at[d], arrived.at[r], disp_s.at[k - 1], disp_r.at[k - 1], {"er": r}).wait_recv()

        return nt(arrived[r], wd[...])

    def keep(d, value):
        part[d, 0] = value[:, :half].astype(BF16)
        part[d, 1] = value[:, half:].astype(BF16)

    keep(2, partial(2))
    rel = [
        remote(part.at[2, 0], relay_in.at[0], rel_s.at[0], rel_r.at[0], right),
        remote(part.at[2, 1], relay_in.at[1], rel_s.at[1], rel_r.at[1], left),
    ]
    for copy in rel:
        copy.start()
    keep(1, partial(1))
    keep(3, partial(3))
    direct = [
        remote(part.at[3, 0], direct_in.at[0], dir_s.at[0], dir_r.at[0], left),
        remote(part.at[1, 1], direct_in.at[1], dir_s.at[1], dir_r.at[1], right),
    ]
    for copy in direct:
        copy.start()
    combined = []
    for h, (d, dev) in enumerate(((1, right), (3, left))):
        rel[h].wait_recv()
        comb[h] = (part[d, h].astype(F32) + relay_in[h].astype(F32)).astype(BF16)
        copy = remote(comb.at[h], comb_in.at[h], com_s.at[h], com_r.at[h], dev)
        copy.start()
        combined.append(copy)
    own[...] = partial(0)

    def outer(q, _):
        total = jnp.dot(hid_t[q, 0], arrived[0], preferred_element_type=F32)
        for r in range(1, N):
            total += jnp.dot(hid_t[q, r], arrived[r], preferred_element_type=F32)
        dn[q] = total.astype(BF16)
        return 0

    lax.fori_loop(0, NX * NC, outer, 0)
    swap = remote(
        dn.at[pl.ds((1 - core) * NX, NX)], cin, core_s, core_r, {"dp": dp_at(x, y, 1 - core)}
    )
    swap.start()

    for h in range(2):
        direct[h].wait_recv()
        combined[h].wait_recv()
        total = own[:, h * half : (h + 1) * half] + direct_in[h].astype(F32) + comb_in[h].astype(F32)
        hid[c, h] = total.astype(BF16)
    first = [
        remote(hid.at[c, 0], hid.at[c, 0], aga_s.at[0], aga_r.at[0], right),
        remote(hid.at[c, 1], hid.at[c, 1], aga_s.at[1], aga_r.at[1], left),
    ]
    second = [
        remote(hid.at[c, 0], hid.at[c, 0], agb_s.at[0], agb_r.at[0], left),
        remote(hid.at[c, 1], hid.at[c, 1], agb_s.at[1], agb_r.at[1], right),
    ]
    for copy in first + second:
        copy.start()

    loads[4].wait()
    loads[5].wait()

    def give_back(d):
        j = (c + d) % N
        r = (j - e + N) % N
        k = (r - e + N) % N
        value = None
        for h in range(2):
            cut = slice(h * half, (h + 1) * half)
            grad = hid[j, h].astype(F32)
            gate_grad = (grad * gfac[r, :, cut]).astype(BF16)
            up_grad = (grad * ufac[r, :, cut]).astype(BF16)
            term = nt(gate_grad, wg[:, cut]) + nt(up_grad, wu[:, cut])
            value = term if value is None else value + term
        slotbuf[d] = value.astype(BF16)

        @pl.when(k == 0)
        def _():
            returned[e] = slotbuf[d]

        @pl.when(k != 0)
        def _():
            remote(slotbuf.at[d], returned.at[e], ret_s.at[k - 1], ret_r.at[k - 1], {"er": r}).start()

    give_back(0)

    swap.wait_recv()
    for q in range(NX):
        xs[q] = (dn[core * NX + q].astype(F32) + cin[q].astype(F32)).astype(BF16)
    over_x = []
    for k in range(1, NX):
        x2 = (x + k) % NX
        copy = remote(
            xs.at[x2], xin.at[k - 1], x_s.at[k - 1], x_r.at[k - 1], {"dp": dp_at(x2, y, core)}
        )
        copy.start()
        over_x.append(copy)

    prev, nxt = (c + 3) % N, (c + 1) % N
    first[0].wait_recv()
    forward = [remote(hid.at[prev, 0], hid.at[prev, 0], agf_s.at[0], agf_r.at[0], right)]
    forward[0].start()
    first[1].wait_recv()
    forward.append(remote(hid.at[nxt, 1], hid.at[nxt, 1], agf_s.at[1], agf_r.at[1], left))
    forward[1].start()
    second[0].wait_recv()
    give_back(1)
    second[1].wait_recv()
    give_back(3)

    for copy in over_x:
        copy.wait_recv()
    total = dn[core * NX + x].astype(F32) + cin[x].astype(F32)
    for k in range(NX - 1):
        total += xin[k].astype(F32)
    ysum[...] = total
    for q in range(NY):
        ys[q] = ysum[q * rows12 : (q + 1) * rows12, :].astype(BF16)
    over_y = []
    for k in range(1, NY):
        y2 = (y + k) % NY
        copy = remote(
            ys.at[y2], yin.at[k - 1], y_s.at[k - 1], y_r.at[k - 1], {"dp": dp_at(x, y2, core)}
        )
        copy.start()
        over_y.append(copy)

    forward[0].wait_recv()
    forward[1].wait_recv()
    give_back(2)

    for copy in over_y:
        copy.wait_recv()
    total = ys[y].astype(F32)
    for k in range(NY - 1):
        total += yin[k].astype(F32)
    down_ref[...] = total * (1.0 / (NX * NY * NC))

    pos_lane = pos_col.astype(jnp.int32) - lax.broadcasted_iota(jnp.int32, (tokens, cap), 1)
    result = None
    for k in range(N):
        source = (e - k + N) % N
        if k > 0:
            remote(
                slotbuf.at[0], returned.at[source], ret_s.at[k - 1], ret_r.at[k - 1], {"er": source}
            ).wait_recv()
        pick = jnp.where(pos_lane == source * cap, 1.0, 0.0).astype(BF16)
        term = jnp.dot(pick, returned[source], preferred_element_type=F32)
        result = term if result is None else result + term
    out_ref[...] = result.astype(BF16)

    for k in range(N - 1):
        other = {"er": (e + k + 1) % N}
        remote(outbuf.at[0], arrived.at[e], disp_s.at[k], disp_r.at[k], other).wait_send()
        remote(slotbuf.at[0], returned.at[e], ret_s.at[k], ret_r.at[k], other).wait_send()
    for copy in rel + direct + combined + first + second + forward + over_x + over_y + [swap]:
        copy.wait_send()


def body(out_grad, route_probs, expert_ids, slot_ids, gate_pre, up_act, w_gate, w_up, w_down):
    tokens, cols = out_grad.shape[1:]
    slots, width = gate_pre.shape[2:]
    cap, half = slots // N, width // 2
    mrows = width // (NX * NC)
    rows12 = mrows // NY
    vmem, dma = pltpu.VMEM, pltpu.SemaphoreType.DMA
    scratch = [
        vmem((tokens, cols), BF16),
        vmem((N, cap, width), BF16),
        vmem((N, cap, width), BF16),
        vmem((cols, width), BF16),
        vmem((cols, width), BF16),
        vmem((width, cols), BF16),
        vmem((N, cap, cols), BF16),
        vmem((N, cap, cols), BF16),
        vmem((N, cap, cols), BF16),
        vmem((N, cap, cols), BF16),
        vmem((N, cap, width), F32),
        vmem((N, cap, width), F32),
        vmem((N, cap, width), BF16),
        vmem((NX * NC, N, mrows, cap), BF16),
        vmem((N, 2, cap, half), BF16),
        vmem((cap, width), F32),
        vmem((2, cap, half), BF16),
        vmem((2, cap, half), BF16),
        vmem((2, cap, half), BF16),
        vmem((2, cap, half), BF16),
        vmem((N, 2, cap, half), BF16),
        vmem((NX * NC, mrows, cols), BF16),
        vmem((NX, mrows, cols), BF16),
        vmem((NX, mrows, cols), BF16),
        vmem((NX - 1, mrows, cols), BF16),
        vmem((mrows, cols), F32),
        vmem((NY, rows12, cols), BF16),
        vmem((NY - 1, rows12, cols), BF16),
        dma((6,)),
        dma((N - 1,)),
        dma((N - 1,)),
        *[dma((2,)) for _ in range(12)],
        dma((N - 1,)),
        dma((N - 1,)),
        dma,
        dma,
        dma((NX - 1,)),
        dma((NX - 1,)),
        dma((NY - 1,)),
        dma((NY - 1,)),
    ]
    small = pl.BlockSpec(memory_space=pltpu.VMEM)
    big = pl.BlockSpec(memory_space=pl.ANY)
    input_grad, down_part = pl.pallas_call(
        kernel,
        out_shape=(
            jax.ShapeDtypeStruct((tokens, cols), BF16),
            jax.ShapeDtypeStruct((rows12, cols), F32),
        ),
        in_specs=[big, small, small, small, big, big, big, big, big],
        out_specs=(small, small),
        scratch_shapes=scratch,
        compiler_params=pltpu.CompilerParams(
            collective_id=0, has_side_effects=True, vmem_limit_bytes=48 * 1024 * 1024
        ),
        name="expert_backward",
    )(
        out_grad[0], route_probs, expert_ids, slot_ids,
        gate_pre.reshape(N, cap, width), up_act.reshape(N, cap, width),
        w_gate[0], w_up[0], w_down[0],
    )
    return (input_grad[None], down_part[None])


def solution(mesh):
    in_specs = (
        P("dp", "er", "ec"),
        P("dp", "er"),
        P("dp", "er"),
        P("dp", "er"),
        P("dp", "er", None, None),
        P("dp", "er", None, None),
        P("er", "ec", None),
        P("er", "ec", None),
        P("er", None, "ec"),
    )
    out_specs = (P("dp", "er", "ec"), P("er", "dp", "ec"))
    return jax.shard_map(body, mesh=mesh, in_specs=in_specs, out_specs=out_specs, check_vma=False)
```

time: 264 us -> 98.2 us (0.37)
  the two profiles are of different devices: /device:TPU:1 before, /device:TPU:2 now
where the time goes in v1:
time: 98.2 us; the launch traced here: 97.8 us
  Pallas kernels  87.8 us (89%)
  local copies, waits for them, and re-layouts  9.37 us (10%)
    pallas_call x1, Pallas kernels, body(): pl.pallas_call(kernel, out_shape=(jax.ShapeDtypeStruct((tokens, cols), BF...  87.8 us
    unnamed x18, local copies, waits for them, and re-layouts  9.37 us

profile of v1, /device:TPU:2, one launch (start us, length us, event | category | flops | bytes accessed | tf_op | source)
XLA Modules:
  0.0 97.8 jit_solution(4548068089561872929)
XLA Ops:
  0.6 0.0 copy-start
  0.6 1.4 %copy-done = bf16[1,1024,768]{2,1,0:T(8,128)(2,1)S(1)} copy-done((bf16[1,1024,768]{2,1,0:T(8,128)(2,1)S(1)}, bf16[1,1024,768]{2,1,0:T(8,128)(2,1)}, u32[]{:S(2)}) %copy-start) | copy-done | bytes 1572888
  2.0 0.0 copy-start.1
  2.0 1.4 %copy-done.1 = bf16[1,1024,768]{2,1,0:T(8,128)(2,1)S(1)} copy-done((bf16[1,1024,768]{2,1,0:T(8,128)(2,1)S(1)}, bf16[1,1024,768]{2,1,0:T(8,128)(2,1)}, u32[]{:S(2)}) %copy-start.1) | copy-done | bytes 1572888
  3.5 0.0 copy-start.2
  3.5 1.0 %copy-done.2 = bf16[1,256,1024]{2,1,0:T(8,128)(2,1)S(1)} copy-done((bf16[1,256,1024]{2,1,0:T(8,128)(2,1)S(1)}, bf16[1,256,1024]{2,1,0:T(8,128)(2,1)}, u32[]{:S(2)}) %copy-start.2) | copy-done | bytes 524312
  4.5 0.0 copy-start.3
  4.5 1.0 %copy-done.3 = bf16[1,1,288,768]{3,2,1,0:T(8,128)(2,1)S(1)} copy-done((bf16[1,1,288,768]{3,2,1,0:T(8,128)(2,1)S(1)}, bf16[1,1,288,768]{3,2,1,0:T(8,128)(2,1)}, u32[]{:S(2)}) %copy-start.3) | copy-done | bytes 442392
  5.5 0.0 copy-start.4
  5.5 1.0 %copy-done.4 = bf16[1,1,288,768]{3,2,1,0:T(8,128)(2,1)S(1)} copy-done((bf16[1,1,288,768]{3,2,1,0:T(8,128)(2,1)S(1)}, bf16[1,1,288,768]{3,2,1,0:T(8,128)(2,1)}, u32[]{:S(2)}) %copy-start.4) | copy-done | bytes 442392
  6.5 0.0 copy-start.5
  6.5 0.7 copy-done.5
  7.2 0.0 copy-start.6
  7.2 0.7 copy-done.6
  7.9 0.0 copy-start.7
  7.9 0.7 copy-done.7
  8.6 87.8 %expert_backward.1 = (bf16[256,1024]{1,0:T(8,128)(2,1)S(1)}, f32[12,1024]{1,0:T(8,128)S(1)}) custom-call(bf16[256,1024]{1,0:T(8,128)(2,1)S(1)} %bitcast.10, f32[1,256]{1,0:T(1,128)S(1)} %copy-done.5, s32[1,256]{1,0:T(1,128)S(1)} %copy-done.6, s32[1,256]{1,0:T(1,128)S(1)} %copy-done.7, bf16[4,72,768]{2,1,0:T(8,128)(2,1)S(1)} %bitcast.12, ...), custom_call_target="tpu_custom_call" | custom-call | tf_op jit(solution)/shard_map/expert_backward/pallas_call | solution.py:343
  96.3 0.7 copy.11
  97.0 0.8 copy.13
Async XLA Ops:
  0.6 1.4 %copy-start = (bf16[1,1024,768]{2,1,0:T(8,128)(2,1)S(1)}, bf16[1,1024,768]{2,1,0:T(8,128)(2,1)}, u32[]{:S(2)}) copy-start(bf16[1,1024,768]{2,1,0:T(8,128)(2,1)} %param.15) | copy-start | bytes 4718596
  2.0 1.4 %copy-start.1 = (bf16[1,1024,768]{2,1,0:T(8,128)(2,1)S(1)}, bf16[1,1024,768]{2,1,0:T(8,128)(2,1)}, u32[]{:S(2)}) copy-start(bf16[1,1024,768]{2,1,0:T(8,128)(2,1)} %param.16) | copy-start | bytes 4718596
  3.5 1.0 %copy-start.2 = (bf16[1,256,1024]{2,1,0:T(8,128)(2,1)S(1)}, bf16[1,256,1024]{2,1,0:T(8,128)(2,1)}, u32[]{:S(2)}) copy-start(bf16[1,256,1024]{2,1,0:T(8,128)(2,1)} %param.9) | copy-start | bytes 1572868
  4.5 1.0 %copy-start.3 = (bf16[1,1,288,768]{3,2,1,0:T(8,128)(2,1)S(1)}, bf16[1,1,288,768]{3,2,1,0:T(8,128)(2,1)}, u32[]{:S(2)}) copy-start(bf16[1,1,288,768]{3,2,1,0:T(8,128)(2,1)} %param.13) | copy-start | bytes 1327108
  5.5 1.0 %copy-start.4 = (bf16[1,1,288,768]{3,2,1,0:T(8,128)(2,1)S(1)}, bf16[1,1,288,768]{3,2,1,0:T(8,128)(2,1)}, u32[]{:S(2)}) copy-start(bf16[1,1,288,768]{3,2,1,0:T(8,128)(2,1)} %param.14) | copy-start | bytes 1327108
  6.5 0.7 copy-start.5
  7.2 0.7 copy-start.6
  7.9 0.7 copy-start.7

commit v2 on v1

--- a/solution.py
+++ b/solution.py
@@ -18,8 +18,9 @@
 
 
 def kernel(
-    tok_hbm, prob_ref, ids_ref, slots_ref, gate_hbm, up_hbm, wg_hbm, wu_hbm, wd_hbm,
+    tok_hbm, prob_hbm, ids_hbm, slots_hbm, gate_hbm, up_hbm, wg_hbm, wu_hbm, wd_hbm,
     out_ref, down_ref,
+    prob_ref, ids_ref, slots_ref,
     tok, gate, up, wg, wu, wd,
     outbuf, arrived, returned, slotbuf,
     gfac, ufac, hidden, hid_t,
@@ -41,11 +42,14 @@
     loads = [
         pltpu.make_async_copy(s, d, lsem.at[i])
         for i, (s, d) in enumerate(
-            [(tok_hbm, tok), (gate_hbm, gate), (up_hbm, up), (wd_hbm, wd), (wg_hbm, wg), (wu_hbm, wu)]
+            [
+                (tok_hbm, tok), (gate_hbm, gate), (up_hbm, up), (wd_hbm, wd), (wg_hbm, wg), (wu_hbm, wu),
+                (ids_hbm, ids_ref), (slots_hbm, slots_ref), (prob_hbm, prob_ref),
+            ]
         )
     ]
-    for load in loads:
-        load.start()
+    for i in (6, 7, 8, 0, 1, 2, 3, 4, 5):
+        loads[i].start()
 
     right, left = {"ec": (c + 1) % N}, {"ec": (c + 3) % N}
     partners = [{"er": (e + k) % N} for k in (1, 2, 3)] + [right, left]
@@ -62,6 +66,8 @@
         )
 
     tokens = tok.shape[0]
+    for i in (6, 7, 8):
+        loads[i].wait()
     pos_row = ids_ref[...] * cap + slots_ref[...]
     eye = lax.broadcasted_iota(jnp.int32, (tokens, tokens), 0) == lax.broadcasted_iota(
         jnp.int32, (tokens, tokens), 1
@@ -172,6 +178,18 @@
         dn.at[pl.ds((1 - core) * NX, NX)], cin, core_s, core_r, {"dp": dp_at(x, y, 1 - core)}
     )
     swap.start()
+
+    swap.wait_recv()
+    for q in range(NX):
+        xs[q] = (dn[core * NX + q].astype(F32) + cin[q].astype(F32)).astype(BF16)
+    over_x = []
+    for k in range(1, NX):
+        x2 = (x + k) % NX
+        copy = remote(
+            xs.at[x2], xin.at[k - 1], x_s.at[k - 1], x_r.at[k - 1], {"dp": dp_at(x2, y, core)}
+        )
+        copy.start()
+        over_x.append(copy)
 
     for h in range(2):
         direct[h].wait_recv()
@@ -215,18 +233,6 @@
             remote(slotbuf.at[d], returned.at[e], ret_s.at[k - 1], ret_r.at[k - 1], {"er": r}).start()
 
     give_back(0)
-
-    swap.wait_recv()
-    for q in range(NX):
-        xs[q] = (dn[core * NX + q].astype(F32) + cin[q].astype(F32)).astype(BF16)
-    over_x = []
-    for k in range(1, NX):
-        x2 = (x + k) % NX
-        copy = remote(
-            xs.at[x2], xin.at[k - 1], x_s.at[k - 1], x_r.at[k - 1], {"dp": dp_at(x2, y, core)}
-        )
-        copy.start()
-        over_x.append(copy)
 
     prev, nxt = (c + 3) % N, (c + 1) % N
     first[0].wait_recv()
@@ -297,6 +303,9 @@
     rows12 = mrows // NY
     vmem, dma = pltpu.VMEM, pltpu.SemaphoreType.DMA
     scratch = [
+        vmem((1, tokens), F32),
+        vmem((1, tokens), jnp.int32),
+        vmem((1, tokens), jnp.int32),
         vmem((tokens, cols), BF16),
         vmem((N, cap, width), BF16),
         vmem((N, cap, width), BF16),
@@ -325,7 +334,7 @@
         vmem((mrows, cols), F32),
         vmem((NY, rows12, cols), BF16),
         vmem((NY - 1, rows12, cols), BF16),
-        dma((6,)),
+        dma((9,)),
         dma((N - 1,)),
         dma((N - 1,)),
         *[dma((2,)) for _ in range(12)],
@@ -339,18 +348,18 @@
         dma((NY - 1,)),
     ]
     small = pl.BlockSpec(memory_space=pltpu.VMEM)
-    big = pl.BlockSpec(memory_space=pl.ANY)
+    big = pl.BlockSpec(memory_space=pltpu.HBM)
     input_grad, down_part = pl.pallas_call(
         kernel,
         out_shape=(
-            jax.ShapeDtypeStruct((tokens, cols), BF16),
-            jax.ShapeDtypeStruct((rows12, cols), F32),
+            pltpu.VMEM((tokens, cols), BF16),
+            pltpu.VMEM((rows12, cols), F32),
         ),
-        in_specs=[big, small, small, small, big, big, big, big, big],
+        in_specs=[big] * 9,
         out_specs=(small, small),
         scratch_shapes=scratch,
         compiler_params=pltpu.CompilerParams(
-            collective_id=0, has_side_effects=True, vmem_limit_bytes=48 * 1024 * 1024
+            collective_id=0, has_side_effects=True, vmem_limit_bytes=58 * 1024 * 1024
         ),
         name="expert_backward",
     )(

time: 98.2 us -> 86.4 us (0.88)
  the two profiles are of different devices: /device:TPU:2 before, /device:TPU:1 now
where the time goes in v2:
time: 86.4 us; the launch traced here: 86.3 us
  Pallas kernels  84.2 us (97%)
  local copies, waits for them, and re-layouts  1.47 us (2%)
    pallas_call x1, Pallas kernels, body(): pl.pallas_call(kernel, out_shape=(pltpu.VMEM((tokens, cols), BF16), pltpu...  84.2 us

profile of v2, /device:TPU:1, one launch (start us, length us, event | category | flops | bytes accessed | tf_op | source)
XLA Modules:
  0.0 86.3 jit_solution(5492898033835376399)
XLA Ops:
  0.6 84.2 %expert_backward.1 = (bf16[256,1024]{1,0:T(8,128)(2,1)S(1)}, f32[12,1024]{1,0:T(8,128)S(1)}) custom-call(bf16[256,1024]{1,0:T(8,128)(2,1)} %bitcast.13, f32[1,256]{1,0:T(1,128)} %prob_hbm.1, s32[1,256]{1,0:T(1,128)} %ids_hbm.1, s32[1,256]{1,0:T(1,128)} %slots_hbm.1, bf16[4,72,768]{2,1,0:T(8,128)(2,1)} %bitcast.14, bf16[4,72,768]{2,1,0:T(8,128)(2,1)} %bitcast.15, ...), custom_call_target="tpu_custom_call" | custom-call | tf_op jit(solution)/shard_map/expert_backward/pallas_call | solution.py:352
  84.8 0.8 copy.13
  85.6 0.7 copy.11

commit v3 on v2

--- a/solution.py
+++ b/solution.py
@@ -65,6 +65,9 @@
             src_ref=src, dst_ref=dst, send_sem=s, recv_sem=r, device_id=dev, device_id_type=MESH
         )
 
+    def arriving(ref, r):
+        remote(ref, ref, r, r, right).wait_recv()
+
     tokens = tok.shape[0]
     for i in (6, 7, 8):
         loads[i].wait()
@@ -157,13 +160,15 @@
     ]
     for copy in direct:
         copy.start()
-    combined = []
-    for h, (d, dev) in enumerate(((1, right), (3, left))):
-        rel[h].wait_recv()
+    for n in range(2):
+        h = jnp.where((c == 0) | (c == N - 1), 1 - n, n)
+        d = 1 + 2 * h
+        arriving(relay_in.at[h], rel_r.at[h])
         comb[h] = (part[d, h].astype(F32) + relay_in[h].astype(F32)).astype(BF16)
-        copy = remote(comb.at[h], comb_in.at[h], com_s.at[h], com_r.at[h], dev)
-        copy.start()
-        combined.append(copy)
+        remote(comb.at[h], comb_in.at[h], com_s.at[h], com_r.at[h], {"ec": (c + d) % N}).start()
+    combined = [
+        remote(comb.at[h], comb_in.at[h], com_s.at[h], com_r.at[h], dev) for h, dev in enumerate((right, left))
+    ]
     own[...] = partial(0)
 
     def outer(q, _):
@@ -191,24 +196,27 @@
         copy.start()
         over_x.append(copy)
 
+    first = [
+        remote(hid.at[c, 0], hid.at[c, 0], aga_s.at[0], aga_r.at[0], right),
+        remote(hid.at[c, 1], hid.at[c, 1], aga_s.at[1], aga_r.at[1], left),
+    ]
+    second = [
+        remote(hid.at[c, 0], hid.at[c, 0], agb_s.at[0], agb_r.at[0], left),
+        remote(hid.at[c, 1], hid.at[c, 1], agb_s.at[1], agb_r.at[1], right),
+    ]
     for h in range(2):
         direct[h].wait_recv()
         combined[h].wait_recv()
         total = own[:, h * half : (h + 1) * half] + direct_in[h].astype(F32) + comb_in[h].astype(F32)
         hid[c, h] = total.astype(BF16)
-    first = [
-        remote(hid.at[c, 0], hid.at[c, 0], aga_s.at[0], aga_r.at[0], right),
-        remote(hid.at[c, 1], hid.at[c, 1], aga_s.at[1], aga_r.at[1], left),
-    ]
-    second = [
-        remote(hid.at[c, 0], hid.at[c, 0], agb_s.at[0], agb_r.at[0], left),
-        remote(hid.at[c, 1], hid.at[c, 1], agb_s.at[1], agb_r.at[1], right),
-    ]
-    for copy in first + second:
+        first[h].start()
+    for copy in second:
         copy.start()
 
     loads[4].wait()
     loads[5].wait()
+
+    early = c < N // 2
 
     def give_back(d):
         j = (c + d) % N
@@ -228,24 +236,27 @@
         def _():
             returned[e] = slotbuf[d]
 
-        @pl.when(k != 0)
-        def _():
-            remote(slotbuf.at[d], returned.at[e], ret_s.at[k - 1], ret_r.at[k - 1], {"er": r}).start()
+        @pl.when((k != 0) & (early | (d == 2)))
+        def _():
+            send_back(d)
+
+    def send_back(d):
+        r = (c + d - e + N) % N
+        k = (r - e + N) % N
+        remote(slotbuf.at[d], returned.at[e], ret_s.at[k - 1], ret_r.at[k - 1], {"er": r}).start()
 
     give_back(0)
 
-    prev, nxt = (c + 3) % N, (c + 1) % N
-    first[0].wait_recv()
-    forward = [remote(hid.at[prev, 0], hid.at[prev, 0], agf_s.at[0], agf_r.at[0], right)]
-    forward[0].start()
-    first[1].wait_recv()
-    forward.append(remote(hid.at[nxt, 1], hid.at[nxt, 1], agf_s.at[1], agf_r.at[1], left))
-    forward[1].start()
-    second[0].wait_recv()
-    give_back(1)
-    second[1].wait_recv()
-    give_back(3)
-
+    for n in range(2):
+        h = jnp.where((c == 1) | (c == 2), 1 - n, n)
+        source = (c + 3 - 2 * h + N) % N
+        arriving(hid.at[source, h], aga_r.at[h])
+        remote(
+            hid.at[source, h], hid.at[source, h], agf_s.at[h], agf_r.at[h], {"ec": (c + 1 + 2 * h) % N}
+        ).start()
+    forward = [
+        remote(hid.at[(c + 2) % N, h], hid.at[(c + 2) % N, h], agf_s.at[h], agf_r.at[h], right) for h in range(2)
+    ]
     for copy in over_x:
         copy.wait_recv()
     total = dn[core * NX + x].astype(F32) + cin[x].astype(F32)
@@ -263,8 +274,19 @@
         copy.start()
         over_y.append(copy)
 
+    second[0].wait_recv()
+    give_back(1)
+    second[1].wait_recv()
+    give_back(3)
+
     forward[0].wait_recv()
     forward[1].wait_recv()
+    for d in (0, 1, 3):
+
+        @pl.when(jnp.logical_not(early) & ((c + d - 2 * e + 2 * N) % N != 0))
+        def _():
+            send_back(d)
+
     give_back(2)
 
     for copy in over_y:

time: 86.4 us -> 86.9 us (level)
  the two profiles are of different devices: /device:TPU:1 before, /device:TPU:2 now
where the time goes in v3:
time: 86.9 us; the launch traced here: 86.7 us
  Pallas kernels  84.6 us (97%)
  local copies, waits for them, and re-layouts  1.47 us (2%)
    pallas_call x1, Pallas kernels, body(): pl.pallas_call(kernel, out_shape=(pltpu.VMEM((tokens, cols), BF16), pltpu...  84.6 us

profile of v3, /device:TPU:2, one launch (start us, length us, event | category | flops | bytes accessed | tf_op | source)
XLA Modules:
  0.0 86.7 jit_solution(2242519737853210948)
XLA Ops:
  0.6 84.6 %expert_backward.1 = (bf16[256,1024]{1,0:T(8,128)(2,1)S(1)}, f32[12,1024]{1,0:T(8,128)S(1)}) custom-call(bf16[256,1024]{1,0:T(8,128)(2,1)} %bitcast.13, f32[1,256]{1,0:T(1,128)} %prob_hbm.1, s32[1,256]{1,0:T(1,128)} %ids_hbm.1, s32[1,256]{1,0:T(1,128)} %slots_hbm.1, bf16[4,72,768]{2,1,0:T(8,128)(2,1)} %bitcast.14, bf16[4,72,768]{2,1,0:T(8,128)(2,1)} %bitcast.15, ...), custom_call_target="tpu_custom_call" | custom-call | tf_op jit(solution)/shard_map/expert_backward/pallas_call | solution.py:374
  85.3 0.8 copy.13
  86.1 0.7 copy.11

commit v4 on v3

--- a/solution.py
+++ b/solution.py
@@ -10,6 +10,7 @@
 MESH = pl.DeviceIdType.MESH
 F32, BF16 = jnp.float32, jnp.bfloat16
 NX, NY, NC = 4, 8, 2
+LIMIT = 58 * 1024 * 1024
 N = 4
 
 
@@ -17,71 +18,57 @@
     return lax.dot_general(a, b, (((1,), (1,)), ((), ())), preferred_element_type=F32)
 
 
-def kernel(
-    tok_hbm, prob_hbm, ids_hbm, slots_hbm, gate_hbm, up_hbm, wg_hbm, wu_hbm, wd_hbm,
-    out_ref, down_ref,
-    prob_ref, ids_ref, slots_ref,
-    tok, gate, up, wg, wu, wd,
-    outbuf, arrived, returned, slotbuf,
-    gfac, ufac, hidden, hid_t,
-    part, own, relay_in, direct_in, comb, comb_in, hid,
-    dn, cin, xs, xin, ysum, ys, yin,
-    lsem, disp_s, disp_r, rel_s, rel_r, dir_s, dir_r, com_s, com_r,
-    aga_s, aga_r, agb_s, agb_r, agf_s, agf_r, ret_s, ret_r,
-    core_s, core_r, x_s, x_r, y_s, y_r,
-):
-    e, c, p = lax.axis_index("er"), lax.axis_index("ec"), lax.axis_index("dp")
-    core, y, x = p % NC, (p // NC) % NY, p // (NC * NY)
-    cap = arrived.shape[1]
-    half = part.shape[3]
-    rows12 = ysum.shape[0] // NY
-
-    def dp_at(x2, y2, core2):
-        return (x2 * NY + y2) * NC + core2
-
-    loads = [
-        pltpu.make_async_copy(s, d, lsem.at[i])
-        for i, (s, d) in enumerate(
-            [
-                (tok_hbm, tok), (gate_hbm, gate), (up_hbm, up), (wd_hbm, wd), (wg_hbm, wg), (wu_hbm, wu),
-                (ids_hbm, ids_ref), (slots_hbm, slots_ref), (prob_hbm, prob_ref),
-            ]
-        )
-    ]
-    for i in (6, 7, 8, 0, 1, 2, 3, 4, 5):
-        loads[i].start()
-
-    right, left = {"ec": (c + 1) % N}, {"ec": (c + 3) % N}
-    partners = [{"er": (e + k) % N} for k in (1, 2, 3)] + [right, left]
-    partners += [{"dp": dp_at(x, y, 1 - core)}]
-    partners += [{"dp": dp_at((x + k) % NX, y, core)} for k in range(1, NX)]
-    partners += [{"dp": dp_at(x, (y + k) % NY, core)} for k in range(1, NY)]
+def remote(src, dst, s, r, dev):
+    return pltpu.make_async_remote_copy(
+        src_ref=src, dst_ref=dst, send_sem=s, recv_sem=r, device_id=dev, device_id_type=MESH
+    )
+
+
+def greet(partners):
     barrier = pltpu.get_barrier_semaphore()
     for partner in partners:
         pl.semaphore_signal(barrier, inc=1, device_id=partner, device_id_type=MESH)
-
-    def remote(src, dst, s, r, dev):
-        return pltpu.make_async_remote_copy(
-            src_ref=src, dst_ref=dst, send_sem=s, recv_sem=r, device_id=dev, device_id_type=MESH
-        )
-
-    def arriving(ref, r):
-        remote(ref, ref, r, r, right).wait_recv()
-
+    return barrier
+
+
+def copies_in(pairs, sems):
+    loads = [pltpu.make_async_copy(s, d, sems.at[i]) for i, (s, d) in enumerate(pairs)]
+    for load in loads:
+        load.start()
+    return loads
+
+
+def as_column(row):
+    n = row.shape[1]
+    eye = lax.broadcasted_iota(jnp.int32, (n, n), 0) == lax.broadcasted_iota(jnp.int32, (n, n), 1)
+    return jnp.sum(jnp.where(eye, jnp.broadcast_to(row, (n, n)), 0.0), axis=1, keepdims=True)
+
+
+def dispatch_kernel(
+    tok_hbm, prob_hbm, ids_hbm, slots_hbm, gate_hbm, up_hbm,
+    arrived, gfac, ufac, hid_t, place,
+    prob_ref, ids_ref, slots_ref, tok, gate, up, outbuf, hidden,
+    lsem, disp_s, disp_r,
+):
+    e, c = lax.axis_index("er"), lax.axis_index("ec")
+    cap = arrived.shape[1]
+    rows12 = hid_t.shape[2] // NY
+    loads = copies_in(
+        [
+            (ids_hbm, ids_ref), (slots_hbm, slots_ref), (prob_hbm, prob_ref),
+            (tok_hbm, tok), (gate_hbm, gate), (up_hbm, up),
+        ],
+        lsem,
+    )
+    others = [{"er": (e + k) % N} for k in range(1, N)]
+    barrier = greet(others)
     tokens = tok.shape[0]
-    for i in (6, 7, 8):
+    for i in range(3):
         loads[i].wait()
     pos_row = ids_ref[...] * cap + slots_ref[...]
-    eye = lax.broadcasted_iota(jnp.int32, (tokens, tokens), 0) == lax.broadcasted_iota(
-        jnp.int32, (tokens, tokens), 1
-    )
-
-    def as_column(row):
-        return jnp.sum(jnp.where(eye, jnp.broadcast_to(row, (tokens, tokens)), 0.0), axis=1, keepdims=True)
-
+    place[...] = pos_row.astype(F32)
     prob_col = as_column(prob_ref[...])
-    pos_col = as_column(pos_row.astype(F32))
-    loads[0].wait()
+    loads[3].wait()
     tok[...] = (prob_col * tok[...].astype(F32)).astype(BF16)
     for n, d in enumerate((2, 1, 3, 0)):
         dest = (c + d - e + 2 * N) % N
@@ -90,7 +77,7 @@
         pick = jnp.where(slot == pos_row, 1.0, 0.0).astype(BF16)
         outbuf[d] = jnp.dot(pick, tok[...], preferred_element_type=F32).astype(BF16)
         if n == 0:
-            pl.semaphore_wait(barrier, len(partners))
+            pl.semaphore_wait(barrier, len(others))
 
         @pl.when(k == 0)
         def _():
@@ -100,8 +87,8 @@
         def _():
             remote(outbuf.at[d], arrived.at[e], disp_s.at[k - 1], disp_r.at[k - 1], {"er": dest}).start()
 
-    loads[1].wait()
-    loads[2].wait()
+    loads[4].wait()
+    loads[5].wait()
 
     def activations(r, _):
         a, u = gate[r].astype(F32), up[r].astype(F32)
@@ -129,23 +116,57 @@
 
     lax.fori_loop(0, NX * NC, arrange, 0)
 
-    loads[3].wait()
+    for k in range(N - 1):
+        source = (e - k - 1 + N) % N
+        remote(outbuf.at[0], arrived.at[source], disp_s.at[k], disp_r.at[k], others[k]).wait()
+
+
+def kernel(
+    arrived, gfac, ufac, hid_t, place, wg_hbm, wu_hbm, wd_hbm,
+    out_ref, down_ref,
+    wg, wu, wd,
+    returned, slotbuf,
+    part, own, relay_in, direct_in, comb, comb_in, hid,
+    dn, cin, xs, xin, ysum, ys, yin,
+    lsem, rel_s, rel_r, dir_s, dir_r, com_s, com_r,
+    aga_s, aga_r, agb_s, agb_r, agf_s, agf_r, ret_s, ret_r,
+    core_s, core_r, x_s, x_r, y_s, y_r,
+):
+    e, c, p = lax.axis_index("er"), lax.axis_index("ec"), lax.axis_index("dp")
+    core, y, x = p % NC, (p // NC) % NY, p // (NC * NY)
+    cap = arrived.shape[1]
+    half = part.shape[3]
+    rows12 = ysum.shape[0] // NY
+    tokens = out_ref.shape[0]
+
+    def dp_at(x2, y2, core2):
+        return (x2 * NY + y2) * NC + core2
+
+    loads = copies_in(
+        [(wd_hbm, wd), (wg_hbm, wg), (wu_hbm, wu)], lsem
+    )
+    right, left = {"ec": (c + 1) % N}, {"ec": (c + 3) % N}
+    partners = [{"er": (e + k) % N} for k in (1, 2, 3)] + [right, left]
+    partners += [{"dp": dp_at(x, y, 1 - core)}]
+    partners += [{"dp": dp_at((x + k) % NX, y, core)} for k in range(1, NX)]
+    partners += [{"dp": dp_at(x, (y + k) % NY, core)} for k in range(1, NY)]
+    barrier = greet(partners)
+
+    def arriving(ref, r):
+        remote(ref, ref, r, r, right).wait_recv()
+
+    loads[0].wait()
 
     def partial(d):
-        r = (c + d - e + 2 * N) % N
-        k = (e - r + N) % N
-
-        @pl.when(k != 0)
-        def _():
-            remote(outbuf.at[d], arrived.at[r], disp_s.at[k - 1], disp_r.at[k - 1], {"er": r}).wait_recv()
-
-        return nt(arrived[r], wd[...])
+        return nt(arrived[(c + d - e + 2 * N) % N], wd[...])
 
     def keep(d, value):
         part[d, 0] = value[:, :half].astype(BF16)
         part[d, 1] = value[:, half:].astype(BF16)
 
     keep(2, partial(2))
+    pos_col = as_column(place[...])
+    pl.semaphore_wait(barrier, len(partners))
     rel = [
         remote(part.at[2, 0], relay_in.at[0], rel_s.at[0], rel_r.at[0], right),
         remote(part.at[2, 1], relay_in.at[1], rel_s.at[1], rel_r.at[1], left),
@@ -213,8 +234,8 @@
     for copy in second:
         copy.start()
 
-    loads[4].wait()
-    loads[5].wait()
+    loads[1].wait()
+    loads[2].wait()
 
     early = c < N // 2
 
@@ -311,7 +332,6 @@
 
     for k in range(N - 1):
         other = {"er": (e + k + 1) % N}
-        remote(outbuf.at[0], arrived.at[e], disp_s.at[k], disp_r.at[k], other).wait_send()
         remote(slotbuf.at[0], returned.at[e], ret_s.at[k], ret_r.at[k], other).wait_send()
     for copy in rel + direct + combined + first + second + forward + over_x + over_y + [swap]:
         copy.wait_send()
@@ -324,30 +344,49 @@
     mrows = width // (NX * NC)
     rows12 = mrows // NY
     vmem, dma = pltpu.VMEM, pltpu.SemaphoreType.DMA
+    small = pl.BlockSpec(memory_space=pltpu.VMEM)
+    big = pl.BlockSpec(memory_space=pl.ANY)
+    handed = pl.pallas_call(
+        dispatch_kernel,
+        out_shape=(
+            vmem((N, cap, cols), BF16),
+            vmem((N, cap, width), F32),
+            vmem((N, cap, width), F32),
+            vmem((NX * NC, N, mrows, cap), BF16),
+            vmem((1, tokens), F32),
+        ),
+        in_specs=[big] * 6,
+        out_specs=(small,) * 5,
+        scratch_shapes=[
+            vmem((1, tokens), F32),
+            vmem((1, tokens), jnp.int32),
+            vmem((1, tokens), jnp.int32),
+            vmem((tokens, cols), BF16),
+            vmem((N, cap, width), BF16),
+            vmem((N, cap, width), BF16),
+            vmem((N, cap, cols), BF16),
+            vmem((N, cap, width), BF16),
+            dma((6,)),
+            dma((N - 1,)),
+            dma((N - 1,)),
+        ],
+        compiler_params=pltpu.CompilerParams(
+            collective_id=1, has_side_effects=True, vmem_limit_bytes=LIMIT
+        ),
+        name="dispatch",
+    )(
+        out_grad[0], route_probs, expert_ids, slot_ids,
+        gate_pre.reshape(N, cap, width), up_act.reshape(N, cap, width),
+    )
     scratch = [
-        vmem((1, tokens), F32),
-        vmem((1, tokens), jnp.int32),
-        vmem((1, tokens), jnp.int32),
-        vmem((tokens, cols), BF16),
-        vmem((N, cap, width), BF16),
-        vmem((N, cap, width), BF16),
         vmem((cols, width), BF16),
         vmem((cols, width), BF16),
         vmem((width, cols), BF16),
         vmem((N, cap, cols), BF16),
         vmem((N, cap, cols), BF16),
-        vmem((N, cap, cols), BF16),
-        vmem((N, cap, cols), BF16),
-        vmem((N, cap, width), F32),
-        vmem((N, cap, width), F32),
-        vmem((N, cap, width), BF16),
-        vmem((NX * NC, N, mrows, cap), BF16),
         vmem((N, 2, cap, half), BF16),
         vmem((cap, width), F32),
-        vmem((2, cap, half), BF16),
-        vmem((2, cap, half), BF16),
-        vmem((2, cap, half), BF16),
-        vmem((2, cap, half), BF16),
+        *[vmem((2, cap, half), BF16) for _ in range(4)],
         vmem((N, 2, cap, half), BF16),
         vmem((NX * NC, mrows, cols), BF16),
         vmem((NX, mrows, cols), BF16),
@@ -356,9 +395,7 @@
         vmem((mrows, cols), F32),
         vmem((NY, rows12, cols), BF16),
         vmem((NY - 1, rows12, cols), BF16),
-        dma((9,)),
-        dma((N - 1,)),
-        dma((N - 1,)),
+        dma((3,)),
         *[dma((2,)) for _ in range(12)],
         dma((N - 1,)),
         dma((N - 1,)),
@@ -369,26 +406,17 @@
         dma((NY - 1,)),
         dma((NY - 1,)),
     ]
-    small = pl.BlockSpec(memory_space=pltpu.VMEM)
-    big = pl.BlockSpec(memory_space=pltpu.HBM)
     input_grad, down_part = pl.pallas_call(
         kernel,
-        out_shape=(
-            pltpu.VMEM((tokens, cols), BF16),
-            pltpu.VMEM((rows12, cols), F32),
-        ),
-        in_specs=[big] * 9,
+        out_shape=(vmem((tokens, cols), BF16), vmem((rows12, cols), F32)),
+        in_specs=[small] * 5 + [big] * 3,
         out_specs=(small, small),
         scratch_shapes=scratch,
         compiler_params=pltpu.CompilerParams(
-            collective_id=0, has_side_effects=True, vmem_limit_bytes=58 * 1024 * 1024
+            collective_id=0, has_side_effects=True, vmem_limit_bytes=LIMIT - 8 * 1024 * 1024
         ),
         name="expert_backward",
-    )(
-        out_grad[0], route_probs, expert_ids, slot_ids,
-        gate_pre.reshape(N, cap, width), up_act.reshape(N, cap, width),
-        w_gate[0], w_up[0], w_down[0],
-    )
+    )(*handed, w_gate[0], w_up[0], w_down[0])
     return (input_grad[None], down_part[None])
 
 

time: 86.9 us -> 89 us (1.024)
  the two profiles are of different devices: /device:TPU:2 before, /device:TPU:14 now
where the time goes in v4:
time: 89 us; the launch traced here: 88.8 us
  Pallas kernels  86.7 us (97%)
  local copies, waits for them, and re-layouts  1.47 us (2%)
    pallas_call x1, Pallas kernels, body(): pl.pallas_call(kernel, out_shape=(vmem((tokens, cols), BF16), vmem((rows1...  69.4 us
    pallas_call x1, Pallas kernels, body(): pl.pallas_call(dispatch_kernel, out_shape=(vmem((N, cap, cols), BF16), vm...  17.3 us

profile of v4, /device:TPU:14, one launch (start us, length us, event | category | flops | bytes accessed | tf_op | source)
XLA Modules:
  0.0 88.8 jit_solution(16918735562540775094)
XLA Ops:
  0.6 17.3 %dispatch.1 = (bf16[4,72,1024]{2,1,0:T(8,128)(2,1)S(1)}, f32[4,72,768]{2,1,0:T(8,128)S(1)}, f32[4,72,768]{2,1,0:T(8,128)S(1)}, bf16[8,4,96,72]{3,2,1,0:T(8,128)(2,1)S(1)}, f32[1,256]{1,0:T(1,128)S(1)}) custom-call(bf16[256,1024]{1,0:T(8,128)(2,1)} %bitcast.13, f32[1,256]{1,0:T(1,128)} %prob_hbm.1, s32[1,256]{1,0:T(1,128)} %ids_hbm.1, s32[1,256]{1,0:T(1,128)} %slots_hbm.1, ...), custom_call_target="tpu_custom_call" | custom-call | tf_op jit(solution)/shard_map/dispatch/pallas_call | solution.py:349
  17.9 69.4 %expert_backward.1 = (bf16[256,1024]{1,0:T(8,128)(2,1)S(1)}, f32[12,1024]{1,0:T(8,128)S(1)}) custom-call(bf16[4,72,1024]{2,1,0:T(8,128)(2,1)S(1)} %get-tuple-element.9.arrived, f32[4,72,768]{2,1,0:T(8,128)S(1)} %get-tuple-element.10.gfac, f32[4,72,768]{2,1,0:T(8,128)S(1)} %get-tuple-element.11.ufac, bf16[8,4,96,72]{3,2,1,0:T(8,128)(2,1)S(1)} %get-tuple-element.12.hid_t, ...), custom_call_target="tpu_custom_call" | custom-call | tf_op jit(solution)/shard_map/expert_backward/pallas_call | solution.py:409
  87.4 0.8 copy.13
  88.2 0.7 copy.11

commit v5 on v3

--- a/solution.py
+++ b/solution.py
@@ -10,6 +10,7 @@
 MESH = pl.DeviceIdType.MESH
 F32, BF16 = jnp.float32, jnp.bfloat16
 NX, NY, NC = 4, 8, 2
+WAVES = 3
 N = 4
 
 
@@ -33,7 +34,13 @@
     e, c, p = lax.axis_index("er"), lax.axis_index("ec"), lax.axis_index("dp")
     core, y, x = p % NC, (p // NC) % NY, p // (NC * NY)
     cap = arrived.shape[1]
-    half = part.shape[3]
+    piece = part.shape[4]
+    half = WAVES * piece
+    pieces = [(h, w) for w in range(WAVES) for h in range(2)]
+
+    def columns(h, w):
+        return slice(h * half + w * piece, h * half + (w + 1) * piece)
+
     rows12 = ysum.shape[0] // NY
 
     def dp_at(x2, y2, core2):
@@ -142,32 +149,33 @@
         return nt(arrived[r], wd[...])
 
     def keep(d, value):
-        part[d, 0] = value[:, :half].astype(BF16)
-        part[d, 1] = value[:, half:].astype(BF16)
+        for h, w in pieces:
+            part[d, h, w] = value[:, columns(h, w)].astype(BF16)
 
     keep(2, partial(2))
     rel = [
-        remote(part.at[2, 0], relay_in.at[0], rel_s.at[0], rel_r.at[0], right),
-        remote(part.at[2, 1], relay_in.at[1], rel_s.at[1], rel_r.at[1], left),
+        remote(part.at[2, h, w], relay_in.at[h, w], rel_s.at[h, w], rel_r.at[h, w], (right, left)[h])
+        for h, w in pieces
     ]
     for copy in rel:
         copy.start()
     keep(1, partial(1))
     keep(3, partial(3))
     direct = [
-        remote(part.at[3, 0], direct_in.at[0], dir_s.at[0], dir_r.at[0], left),
-        remote(part.at[1, 1], direct_in.at[1], dir_s.at[1], dir_r.at[1], right),
+        remote(part.at[3 - 2 * h, h, w], direct_in.at[h, w], dir_s.at[h, w], dir_r.at[h, w], (left, right)[h])
+        for h, w in pieces
     ]
     for copy in direct:
         copy.start()
-    for n in range(2):
+    for n, w in pieces:
         h = jnp.where((c == 0) | (c == N - 1), 1 - n, n)
         d = 1 + 2 * h
-        arriving(relay_in.at[h], rel_r.at[h])
-        comb[h] = (part[d, h].astype(F32) + relay_in[h].astype(F32)).astype(BF16)
-        remote(comb.at[h], comb_in.at[h], com_s.at[h], com_r.at[h], {"ec": (c + d) % N}).start()
+        arriving(relay_in.at[h, w], rel_r.at[h, w])
+        comb[h, w] = (part[d, h, w].astype(F32) + relay_in[h, w].astype(F32)).astype(BF16)
+        remote(comb.at[h, w], comb_in.at[h, w], com_s.at[h, w], com_r.at[h, w], {"ec": (c + d) % N}).start()
     combined = [
-        remote(comb.at[h], comb_in.at[h], com_s.at[h], com_r.at[h], dev) for h, dev in enumerate((right, left))
+        remote(comb.at[h, w], comb_in.at[h, w], com_s.at[h, w], com_r.at[h, w], (right, left)[h])
+        for h, w in pieces
     ]
     own[...] = partial(0)
 
@@ -197,26 +205,25 @@
         over_x.append(copy)
 
     first = [
-        remote(hid.at[c, 0], hid.at[c, 0], aga_s.at[0], aga_r.at[0], right),
-        remote(hid.at[c, 1], hid.at[c, 1], aga_s.at[1], aga_r.at[1], left),
+        remote(hid.at[c, h, w], hid.at[c, h, w], aga_s.at[h, w], aga_r.at[h, w], (right, left)[h])
+        for h, w in pieces
     ]
     second = [
-        remote(hid.at[c, 0], hid.at[c, 0], agb_s.at[0], agb_r.at[0], left),
-        remote(hid.at[c, 1], hid.at[c, 1], agb_s.at[1], agb_r.at[1], right),
-    ]
-    for h in range(2):
-        direct[h].wait_recv()
-        combined[h].wait_recv()
-        total = own[:, h * half : (h + 1) * half] + direct_in[h].astype(F32) + comb_in[h].astype(F32)
-        hid[c, h] = total.astype(BF16)
-        first[h].start()
-    for copy in second:
-        copy.start()
+        remote(hid.at[c, h, w], hid.at[c, h, w], agb_s.at[h, w], agb_r.at[h, w], (left, right)[h])
+        for h, w in pieces
+    ]
+    for i, (h, w) in enumerate(pieces):
+        direct[i].wait_recv()
+        combined[i].wait_recv()
+        total = own[:, columns(h, w)] + direct_in[h, w].astype(F32) + comb_in[h, w].astype(F32)
+        hid[c, h, w] = total.astype(BF16)
+        first[i].start()
+        if h == 1:
+            second[i - 1].start()
+            second[i].start()
 
     loads[4].wait()
     loads[5].wait()
-
-    early = c < N // 2
 
     def give_back(d):
         j = (c + d) % N
@@ -225,7 +232,7 @@
         value = None
         for h in range(2):
             cut = slice(h * half, (h + 1) * half)
-            grad = hid[j, h].astype(F32)
+            grad = jnp.concatenate([hid[j, h, w] for w in range(WAVES)], axis=1).astype(F32)
             gate_grad = (grad * gfac[r, :, cut]).astype(BF16)
             up_grad = (grad * ufac[r, :, cut]).astype(BF16)
             term = nt(gate_grad, wg[:, cut]) + nt(up_grad, wu[:, cut])
@@ -236,7 +243,7 @@
         def _():
             returned[e] = slotbuf[d]
 
-        @pl.when((k != 0) & (early | (d == 2)))
+        @pl.when(k != 0)
         def _():
             send_back(d)
 
@@ -247,15 +254,14 @@
 
     give_back(0)
 
-    for n in range(2):
+    for n, w in pieces:
         h = jnp.where((c == 1) | (c == 2), 1 - n, n)
-        source = (c + 3 - 2 * h + N) % N
-        arriving(hid.at[source, h], aga_r.at[h])
-        remote(
-            hid.at[source, h], hid.at[source, h], agf_s.at[h], agf_r.at[h], {"ec": (c + 1 + 2 * h) % N}
-        ).start()
+        block = hid.at[(c + 3 - 2 * h + N) % N, h, w]
+        arriving(block, aga_r.at[h, w])
+        remote(block, block, agf_s.at[h, w], agf_r.at[h, w], {"ec": (c + 1 + 2 * h) % N}).start()
+    far = (c + 2) % N
     forward = [
-        remote(hid.at[(c + 2) % N, h], hid.at[(c + 2) % N, h], agf_s.at[h], agf_r.at[h], right) for h in range(2)
+        remote(hid.at[far, h, w], hid.at[far, h, w], agf_s.at[h, w], agf_r.at[h, w], right) for h, w in pieces
     ]
     for copy in over_x:
         copy.wait_recv()
@@ -274,19 +280,17 @@
         copy.start()
         over_y.append(copy)
 
-    second[0].wait_recv()
+    for i, (h, _) in enumerate(pieces):
+        if h == 0:
+            second[i].wait_recv()
     give_back(1)
-    second[1].wait_recv()
+    for i, (h, _) in enumerate(pieces):
+        if h == 1:
+            second[i].wait_recv()
     give_back(3)
 
-    forward[0].wait_recv()
-    forward[1].wait_recv()
-    for d in (0, 1, 3):
-
-        @pl.when(jnp.logical_not(early) & ((c + d - 2 * e + 2 * N) % N != 0))
-        def _():
-            send_back(d)
-
+    for copy in forward:
+        copy.wait_recv()
     give_back(2)
 
     for copy in over_y:
@@ -342,13 +346,13 @@
         vmem((N, cap, width), F32),
         vmem((N, cap, width), BF16),
         vmem((NX * NC, N, mrows, cap), BF16),
-        vmem((N, 2, cap, half), BF16),
+        vmem((N, 2, WAVES, cap, half // WAVES), BF16),
         vmem((cap, width), F32),
-        vmem((2, cap, half), BF16),
-        vmem((2, cap, half), BF16),
-        vmem((2, cap, half), BF16),
-        vmem((2, cap, half), BF16),
-        vmem((N, 2, cap, half), BF16),
+        vmem((2, WAVES, cap, half // WAVES), BF16),
+        vmem((2, WAVES, cap, half // WAVES), BF16),
+        vmem((2, WAVES, cap, half // WAVES), BF16),
+        vmem((2, WAVES, cap, half // WAVES), BF16),
+        vmem((N, 2, WAVES, cap, half // WAVES), BF16),
         vmem((NX * NC, mrows, cols), BF16),
         vmem((NX, mrows, cols), BF16),
         vmem((NX, mrows, cols), BF16),
@@ -359,7 +363,7 @@
         dma((9,)),
         dma((N - 1,)),
         dma((N - 1,)),
-        *[dma((2,)) for _ in range(12)],
+        *[dma((2, WAVES)) for _ in range(12)],
         dma((N - 1,)),
         dma((N - 1,)),
         dma,

time: 86.9 us -> 87.1 us (level)
  the two profiles are of different devices: /device:TPU:2 before, /device:TPU:12 now
where the time goes in v5:
time: 87.1 us; the launch traced here: 86.9 us
  Pallas kernels  84.8 us (97%)
  local copies, waits for them, and re-layouts  1.47 us (2%)
    pallas_call x1, Pallas kernels, body(): pl.pallas_call(kernel, out_shape=(pltpu.VMEM((tokens, cols), BF16), pltpu...  84.8 us

profile of v5, /device:TPU:12, one launch (start us, length us, event | category | flops | bytes accessed | tf_op | source)
XLA Modules:
  0.0 86.9 jit_solution(6568523619659679173)
XLA Ops:
  0.6 84.8 %expert_backward.1 = (bf16[256,1024]{1,0:T(8,128)(2,1)S(1)}, f32[12,1024]{1,0:T(8,128)S(1)}) custom-call(bf16[256,1024]{1,0:T(8,128)(2,1)} %bitcast.13, f32[1,256]{1,0:T(1,128)} %prob_hbm.1, s32[1,256]{1,0:T(1,128)} %ids_hbm.1, s32[1,256]{1,0:T(1,128)} %slots_hbm.1, bf16[4,72,768]{2,1,0:T(8,128)(2,1)} %bitcast.14, bf16[4,72,768]{2,1,0:T(8,128)(2,1)} %bitcast.15, ...), custom_call_target="tpu_custom_call" | custom-call | tf_op jit(solution)/shard_map/expert_backward/pallas_call | solution.py:378
  85.4 0.8 copy.13
  86.2 0.7 copy.11
